TPU v7x, 32 devices: a whole 2x2x4 slice. The times are simulated.
32 devices in a mesh: row: 8 (over z, core), col: 4 (over y, x).
Axes of the slice: x: 2, y: 2, z: 4, core: 2. Of those that a mesh axis runs over, the one named last changes fastest.
Arguments:
- act_codes: int32 [512, 7168], P('col', 'row'), may hold values from -127 to 127
- act_scales: float32 [512, 112], P('col', 'row'), may hold values from 0.005 to 0.03
- gate_weight: bfloat16 [7168, 18432], P('row', 'col'), may hold values from -0.0625 to 0.0625
- up_weight: bfloat16 [7168, 18432], P('row', 'col'), may hold values from -0.0625 to 0.0625
- down_weight: bfloat16 [18432, 7168], P('col', 'row'), may hold values from -0.046875 to 0.046875
Outputs:
- mixed: bfloat16 [512, 7168], P('col', 'row')
All inputs are finite; a program needn't handle non-finite values.
Results may differ from a plain program's by a relative error of at most 0.03.
Values may be sent and summed in bfloat16 or wider, within the bound.
A program may use at most 128 MiB of HBM per device.

v0:
```python
import jax
import jax.numpy as jnp
from jax import lax
from jax.sharding import PartitionSpec as P


def on_device(act_codes, act_scales, gate_weight, up_weight, down_weight):
    local_rows = act_codes.shape[0]
    width = act_codes.shape[1]
    nblocks = act_scales.shape[1]
    blocked = act_codes.astype(jnp.float32).reshape(local_rows, nblocks, width // nblocks)
    acts = (blocked * act_scales[:, :, None]).reshape(local_rows, width).astype(jnp.bfloat16)
    every = lax.all_gather(acts, "col", axis=0, tiled=True)
    hidden_width = gate_weight.shape[1]
    gate_part = jnp.dot(every, gate_weight, preferred_element_type=jnp.float32)
    up_part = jnp.dot(every, up_weight, preferred_element_type=jnp.float32)
    summed = lax.psum_scatter(
        jnp.concatenate([gate_part, up_part], axis=1).astype(jnp.bfloat16),
        "row",
        scatter_dimension=0,
        tiled=True,
    ).astype(jnp.float32)
    hidden = (jax.nn.silu(summed[:, :hidden_width]) * summed[:, hidden_width:]).astype(jnp.bfloat16)
    partial_value = jnp.dot(
        lax.all_gather(hidden, "row", axis=0, tiled=True),
        down_weight,
        preferred_element_type=jnp.float32,
    )
    mixed = lax.psum_scatter(
        partial_value.astype(jnp.bfloat16), "col", scatter_dimension=0, tiled=True
    )
    return mixed


def solution(mesh):
    placed = (P("col", "row"), P("col", "row"), P("row", "col"), P("row", "col"), P("col", "row"))
    return jax.shard_map(
        on_device, mesh=mesh, in_specs=placed, out_specs=P("col", "row"), check_vma=False
    )
```

profile of v0, /device:TPU:0, one launch (start us, length us, event | category | flops | bytes accessed | tf_op | source)
XLA Modules:
  0.0 236.7 jit_solution(11513722934624598675)
XLA Ops:
  6.5 0.0 reduce-scatter.3.cloned.1.call-start
  6.5 1.2 copy.7
  7.8 0.7 fusion.1
  8.5 0.0 slice-start
  8.5 14.2 %all_gather.6 = bf16[512,896]{0,1:T(8,128)(2,1)S(1)} all-gather(bf16[128,896]{0,1:T(8,128)(2,1)S(1)} %fusion.1), channel_id=1, replica_groups=mesh['row'=8,'col'=4] {'col'}, dimensions={0}, use_global_device_ids=true | all-gather | bytes 1146880 | tf_op jit(solution)/shard_map/all_gather | solution.py:13
  22.7 0.0 slice-start.1
  22.7 8.8 %convolution_convert_fusion = bf16[512,4608]{1,0:T(8,128)(2,1)S(1)} fusion(bf16[512,896]{0,1:T(8,128)(2,1)S(1)} %all_gather.6, bf16[896,4608]{1,0:T(8,128)(2,1)} %param.8), kind=kOutput, calls=%fused_computation.1 | convolution fusion | flops 4230217728 | bytes 13893632 | tf_op jit(solution)/shard_map/dot_general | solution.py:16
  31.5 0.0 slice-done
  31.5 0.0 slice-done.1
  31.6 5.4 %convolution_convert_fusion.1 = bf16[512,4608]{1,0:T(8,128)(2,1)S(1)} fusion(bf16[512,896]{0,1:T(8,128)(2,1)S(1)} %all_gather.6, bf16[896,4608]{1,0:T(8,128)(2,1)S(1)} %bitcast.11), kind=kOutput, calls=%fused_computation.2 | convolution fusion | flops 4230217728 | bytes 13893632 | tf_op jit(solution)/shard_map/dot_general | solution.py:15
  37.0 4.8 %pad_maximum_fusion = bf16[512,9216]{1,0:T(8,128)(2,1)} fusion(bf16[512,4608]{1,0:T(8,128)(2,1)S(1)} %convolution_convert_fusion, bf16[512,4608]{1,0:T(8,128)(2,1)S(1)} %convolution_convert_fusion.1), kind=kLoop, calls=%fused_computation | loop fusion | flops 18874368 | bytes 18874368 | tf_op jit(solution)/shard_map/concatenate | solution.py:18
  41.8 0.0 reduce-scatter.3.cloned.1.call-update
  41.8 0.0 all-gather.2.cloned.1.call-start
  41.9 99.8 %reduce-scatter.3.cloned.1.call-done = bf16[64,9216]{1,0:T(8,128)(2,1)} async-done(((bf16[512,9216]{1,0:T(8,128)(2,1)}), bf16[64,9216]{1,0:T(8,128)(2,1)}) %reduce-scatter.3.cloned.1.call-update) | async-done | bytes 1179664 | tf_op jit(solution)/shard_map/reduce_scatter | solution.py:17
  141.7 1.4 convert_element_type.18
  143.1 1.2 fusion
  144.3 0.0 all-gather.2.cloned.1.call-update
  144.3 0.0 reduce-scatter.5.cloned.1.call-start
  144.3 49.8 %all-gather.2.cloned.1.call-done = bf16[512,4608]{1,0:T(8,128)(2,1)} async-done(((bf16[64,4608]{1,0:T(8,128)(2,1)}), bf16[512,4608]{1,0:T(8,128)(2,1)}) %all-gather.2.cloned.1.call-update) | async-done | bytes 4718608 | tf_op jit(solution)/shard_map/all_gather | solution.py:25
  194.1 10.1 %convolution_convert_fusion.2 = bf16[512,896]{1,0:T(8,128)(2,1)} fusion(bf16[512,4608]{1,0:T(8,128)(2,1)} %all-gather.2.cloned.1.call-done, bf16[4608,896]{1,0:T(8,128)(2,1)} %param.9), kind=kOutput, calls=%fused_computation.3 | convolution fusion | flops 4228317184 | bytes 13893632 | tf_op jit(solution)/shard_map/dot_general | solution.py:24
  204.2 0.0 reduce-scatter.5.cloned.1.call-update
  204.2 26.0 %reduce-scatter.5.cloned.1.call-done = bf16[128,896]{1,0:T(8,128)(2,1)} async-done(((bf16[512,896]{1,0:T(8,128)(2,1)}), bf16[128,896]{1,0:T(8,128)(2,1)}) %reduce-scatter.5.cloned.1.call-update) | async-done | bytes 229392 | tf_op jit(solution)/shard_map/reduce_scatter | solution.py:29
  (1 shorter events, 0.0 us)
Async XLA Ops:
  6.5 135.2 %reduce-scatter.3.cloned.1.call-start = ((), (), s32[]{:S(2)}) async-start(), calls=%async_computation.2 | async-start | bytes 10616832 | tf_op jit(solution)/shard_map/reduce_scatter | solution.py:17
  8.5 23.0 %slice-start = ((s8[8257536]{0:T(1024)(128)(4,1)}), s8[4194304]{0:T(1024)(128)(4,1)S(1)}, s32[]{:S(2)}) async-start(s8[8257536]{0:T(1024)(128)(4,1)} %bitcast.10), calls=%async_computation.5 | async-start | bytes 8388608
  22.7 8.8 %slice-start.1 = ((s8[8257536]{0:T(1024)(128)(4,1)}), s8[4063232]{0:T(1024)(128)(4,1)S(1)}, s32[]{:S(2)}) async-start(s8[8257536]{0:T(1024)(128)(4,1)} %bitcast.10), calls=%async_computation.6 | async-start | bytes 8126464
  41.8 152.3 %all-gather.2.cloned.1.call-start = ((), (), s32[]{:S(2)}) async-start(), calls=%async_computation.3 | async-start | bytes 5308416 | tf_op jit(solution)/shard_map/all_gather | solution.py:25
  144.3 85.9 %reduce-scatter.5.cloned.1.call-start = ((), (), s32[]{:S(2)}) async-start(), calls=%async_computation.4 | async-start | bytes 1146880 | tf_op jit(solution)/shard_map/reduce_scatter | solution.py:29
Sparse Core Ops, SparseCore 0:
  41.9 99.7 reduce-scatter.2
  144.4 49.6 all-gather.1
  204.4 25.8 reduce-scatter.4
where the time goes:
time: 237 us
  waiting for transfers between devices  176 us (74%)
  matrix products  24.3 us (10%)
  blocking collectives  14.2 us (6%)
  between operations  13.2 us (6%)
  other arithmetic  8.09 us (3%)
    reduce_scatter x1, waiting for transfers between devices, on_device(): lax.psum_scatter(jnp.concatenate([gate_part, up_part], axis=1).astype(jnp...  99.8 us
    all_gather x1, waiting for transfers between devices, on_device(): lax.all_gather(hidden, 'row', axis=0, tiled=True)  49.8 us
    reduce_scatter x1, waiting for transfers between devices, on_device(): lax.psum_scatter(partial_value.astype(jnp.bfloat16), 'col', scatter_dimen...  26 us
    all_gather x1, blocking collectives, on_device(): every = lax.all_gather(acts, 'col', axis=0, tiled=True)  14.2 us
    dot_general x1, matrix products, on_device(): jnp.dot(lax.all_gather(hidden, 'row', axis=0, tiled=True), down_weight, p...  10.1 us
    dot_general x1, matrix products, on_device(): up_part = jnp.dot(every, up_weight, preferred_element_type=jnp.float32)  8.82 us
    dot_general x1, matrix products, on_device(): gate_part = jnp.dot(every, gate_weight, preferred_element_type=jnp.float32)  5.45 us
    concatenate x1, other arithmetic, on_device(): jnp.concatenate([gate_part, up_part], axis=1).astype(jnp.bfloat16)  4.77 us
  transfers between devices with their start and end apart: 3, of which 3 were waited for; matrix products, arithmetic and copies ran while one was open for 0% of the time, Pallas kernels for 0%

commit v1 on v0

v1 whole, which is shorter than its diff:
```python
import functools

import jax
import jax.numpy as jnp
from jax import lax
from jax.experimental import pallas as pl
from jax.experimental.pallas import tpu as pltpu
from jax.sharding import PartitionSpec as P

MESH = pl.DeviceIdType.MESH
GROUPS = 2
WIDTHS = (256, 384, 128)
AHEAD = 2
ROWS_PER_DOT = 256
HOP_STEPS = 2


def body(
    n_row, n_col, x_ref, gate_hbm, up_hbm, down_hbm, o_ref,
    every, gate_w, up_w, down_w, part, from_core, from_chip, hid, acc, out_send, out_recv,
    w_sem, act_s, act_r, core_s, core_r, chip_s, chip_r, hz_s, hz_r, hc_s, hc_r, out_s, out_r,
):
    groups, _, piece, depth = x_ref.shape
    chunks, _, width = gate_w.shape
    steps = groups * chunks
    n_chip = n_row // 2
    rows = n_col * piece

    row, col = lax.axis_index("row"), lax.axis_index("col")
    chip, core = row // 2, row % 2
    pos = jnp.where(core == 0, chip, n_chip - 1 - chip)
    ahead_row = row + jnp.where(core == 0, 2, -2)
    behind_row = row - jnp.where(core == 0, 2, -2)
    other_row = chip * 2 + 1 - core
    is_first, is_last = pos == 0, pos == n_chip - 1

    def weight_copy(kind, j):
        columns = pl.ds(j * width, width)
        if kind == 0:
            return pltpu.make_async_copy(gate_hbm.at[:, columns], gate_w.at[j], w_sem.at[0, j])
        if kind == 1:
            return pltpu.make_async_copy(up_hbm.at[:, columns], up_w.at[j], w_sem.at[1, j])
        return pltpu.make_async_copy(down_hbm.at[columns, :], down_w.at[j], w_sem.at[2, j])

    for j in range(chunks):
        weight_copy(0, j).start()
        weight_copy(1, j).start()

    barrier = pltpu.get_barrier_semaphore()
    for p in range(1, n_col):
        pl.semaphore_signal(barrier, inc=1, device_id={"col": lax.rem(col + p, n_col)}, device_id_type=MESH)
    pl.semaphore_signal(barrier, inc=1, device_id={"row": other_row}, device_id_type=MESH)

    @pl.when(chip > 0)
    def _():
        pl.semaphore_signal(barrier, inc=1, device_id={"row": row - 2}, device_id_type=MESH)

    @pl.when(chip < n_chip - 1)
    def _():
        pl.semaphore_signal(barrier, inc=1, device_id={"row": row + 2}, device_id_type=MESH)

    neighbours = jnp.where(chip > 0, 1, 0) + jnp.where(chip < n_chip - 1, 1, 0)
    pl.semaphore_wait(barrier, n_col + neighbours)

    def remote(src, dst, send, recv, where):
        return pltpu.make_async_remote_copy(
            src_ref=src, dst_ref=dst, send_sem=send, recv_sem=recv, device_id=where, device_id_type=MESH
        )

    def act_copy(g, p):
        return remote(
            x_ref.at[g], every.at[g, :, col], act_s.at[g, p], act_r.at[g, col], {"col": lax.rem(col + p, n_col)}
        )

    def act_arrival(g, p):
        source = lax.rem(col + p, n_col)
        return remote(x_ref.at[g], every.at[g, :, source], act_s.at[g, p], act_r.at[g, source], {"col": source})

    def core_copy(j):
        return remote(part.at[j, 1 - core], from_core.at[j], core_s.at[j], core_r.at[j], {"row": other_row})

    def chip_copy(j):
        return remote(part.at[j, core], from_chip.at[j], chip_s.at[j], chip_r.at[j], {"row": ahead_row})

    def hidden_back(j):
        return remote(hid.at[j, core], hid.at[j, core], hz_s.at[j], hz_r.at[j], {"row": behind_row})

    def hidden_across(j):
        return remote(hid.at[j, core], hid.at[j, core], hc_s.at[j], hc_r.at[j], {"row": other_row})

    def hidden_crossed(j):
        return remote(hid.at[j, 1 - core], hid.at[j, 1 - core], hc_s.at[j], hc_r.at[j], {"row": other_row})

    def out_copy(g, p):
        peer = lax.rem(col + p, n_col)
        return remote(out_send.at[g, peer], out_recv.at[g, col], out_s.at[g, p], out_r.at[g, col], {"col": peer})

    def out_arrival(g, p):
        source = lax.rem(col + p, n_col)
        return remote(out_send.at[g, source], out_recv.at[g, source], out_s.at[g, p], out_r.at[g, source], {"col": source})

    for g in range(groups):
        for p in range(1, n_col):
            act_copy(g, p).start()
        for side in range(2):
            every[g, side, col] = x_ref[g, side]
    for j in range(chunks):
        weight_copy(2, j).start()
    acc[...] = jnp.zeros_like(acc)

    tile = min(ROWS_PER_DOT, 2 * rows)
    side_tile = min(tile, rows)

    def multiply(j):
        g, jj = j // chunks, lax.rem(j, chunks)

        @pl.when(jj == 0)
        def _():
            for p in range(1, n_col):
                act_arrival(g, p).wait_recv()

        @pl.when(g == 0)
        def _():
            weight_copy(0, jj).wait()
            weight_copy(1, jj).wait()

        taken = tile // piece
        for side_at in range(0, 2 * n_col, taken):
            if taken > n_col:
                x = every[g].reshape(2 * rows, depth)
            else:
                x = every[g, side_at // n_col, side_at % n_col:side_at % n_col + taken].reshape(tile, depth)
            for half, w in enumerate((gate_w, up_w)):
                y = jnp.dot(x, w[jj], preferred_element_type=jnp.float32).astype(jnp.bfloat16)
                lanes = slice(half * width, (half + 1) * width)
                if taken > n_col:
                    part[j, :, :, lanes] = y.reshape(2, rows, width)
                else:
                    first = (side_at % n_col) * piece
                    part[j, side_at // n_col, first:first + tile, lanes] = y
        core_copy(j).start()

    def add_up(j):
        core_copy(j).wait_recv()

        @pl.when(is_first)
        def _():
            for r in range(0, rows, side_tile):
                at = slice(r, r + side_tile)
                part[j, core, at] = (
                    part[j, core, at].astype(jnp.float32) + from_core[j, at].astype(jnp.float32)
                ).astype(jnp.bfloat16)
            chip_copy(j).start()

        @pl.when(jnp.logical_not(is_first))
        def _():
            chip_copy(j).wait_recv()

        @pl.when(jnp.logical_not(is_first) & jnp.logical_not(is_last))
        def _():
            for r in range(0, rows, side_tile):
                at = slice(r, r + side_tile)
                part[j, core, at] = (
                    part[j, core, at].astype(jnp.float32)
                    + from_core[j, at].astype(jnp.float32)
                    + from_chip[j, at].astype(jnp.float32)
                ).astype(jnp.bfloat16)
            chip_copy(j).start()

        @pl.when(is_last)
        def _():
            for r in range(0, rows, side_tile):
                at = slice(r, r + side_tile)

                def total(lanes):
                    return (
                        part[j, core, at, lanes].astype(jnp.float32)
                        + from_core[j, at, lanes].astype(jnp.float32)
                        + from_chip[j, at, lanes].astype(jnp.float32)
                    )

                gate, up = total(slice(0, width)), total(slice(width, 2 * width))
                hid[j, core, at] = (gate / (1.0 + jnp.exp(-gate)) * up).astype(jnp.bfloat16)
            hidden_back(j).start()
            hidden_across(j).start()

    def pass_on(j):
        hidden_back(j).wait_recv()

        @pl.when(jnp.logical_not(is_first))
        def _():
            hidden_back(j).start()

        hidden_across(j).start()

    def multiply_down(j):
        jj = lax.rem(j, chunks)
        hidden_crossed(j).wait_recv()

        @pl.when(j < chunks)
        def _():
            weight_copy(2, jj).wait()

        for r in range(0, 2 * rows, tile):
            if tile > rows:
                h = hid[j].reshape(2 * rows, width)
            else:
                h = hid[j, r // rows, r % rows:r % rows + tile]
            acc[r:r + tile] += jnp.dot(h, down_w[jj], preferred_element_type=jnp.float32)

    def hand_out(g):
        for side in range(2):
            for k in range(n_col):
                first = side * rows + k * piece
                out_send[g, k, side] = acc[first:first + piece].astype(jnp.bfloat16)
        acc[...] = jnp.zeros_like(acc)
        for p in range(1, n_col):
            out_copy(g, p).start()

    lag = jnp.maximum(HOP_STEPS * 2 * (n_chip - 1 - pos), 1)
    down_lag = jnp.maximum(lag, HOP_STEPS * (n_chip - 1) + 1)

    early = AHEAD + HOP_STEPS * jnp.maximum(2 * pos - (n_chip - 1), 0)
    early = jnp.minimum(early, steps)

    def begin(j, carry):
        multiply(j)
        return carry

    lax.fori_loop(0, early, begin, 0)

    def step(i, carry):
        @pl.when(i + early < steps)
        def _():
            multiply(i + early)

        @pl.when(i < steps)
        def _():
            add_up(i)

        @pl.when((i >= lag) & (i - lag < steps) & jnp.logical_not(is_last))
        def _():
            pass_on(i - lag)

        @pl.when(i >= down_lag)
        def _():
            j = i - down_lag
            multiply_down(j)

            @pl.when(lax.rem(j, chunks) == chunks - 1)
            def _():
                hand_out(j // chunks)

        return carry

    lax.fori_loop(0, steps + down_lag, step, 0)

    for g in range(groups):
        for p in range(1, n_col):
            out_arrival(g, p).wait_recv()
        for side in range(2):
            total = out_send[g, col, side].astype(jnp.float32)
            for p in range(1, n_col):
                total += out_recv[g, lax.rem(col + p, n_col), side].astype(jnp.float32)
            o_ref[g, side] = total.astype(o_ref.dtype)

    def drain(j, carry):
        core_copy(j).wait_send()
        hidden_across(j).wait_send()

        @pl.when(jnp.logical_not(is_last))
        def _():
            chip_copy(j).wait_send()

        @pl.when(jnp.logical_not(is_first))
        def _():
            hidden_back(j).wait_send()

        return carry

    lax.fori_loop(0, steps, drain, 0)
    for g in range(groups):
        for p in range(1, n_col):
            act_copy(g, p).wait_send()
            out_copy(g, p).wait_send()


def on_device(n_row, n_col, act_codes, act_scales, gate_weight, up_weight, down_weight):
    tokens, depth = act_codes.shape
    nblocks = act_scales.shape[1]
    hidden, out_width = down_weight.shape
    blocked = act_codes.astype(jnp.float32).reshape(tokens, nblocks, depth // nblocks)
    acts = (blocked * act_scales[:, :, None]).reshape(tokens, depth).astype(jnp.bfloat16)

    groups = GROUPS
    piece = tokens // (2 * groups)
    width = next(w for w in WIDTHS if hidden % w == 0)
    chunks = hidden // width
    steps = groups * chunks
    rows = n_col * piece
    bf16 = jnp.bfloat16
    dma = pltpu.SemaphoreType.DMA
    out = pl.pallas_call(
        functools.partial(body, n_row, n_col),
        out_shape=jax.ShapeDtypeStruct((groups, 2, piece, out_width), bf16),
        in_specs=[pl.BlockSpec(memory_space=pltpu.VMEM)] + [pl.BlockSpec(memory_space=pl.ANY)] * 3,
        out_specs=pl.BlockSpec(memory_space=pltpu.VMEM),
        scratch_shapes=[
            pltpu.VMEM((groups, 2, n_col, piece, depth), bf16),
            pltpu.VMEM((chunks, depth, width), bf16),
            pltpu.VMEM((chunks, depth, width), bf16),
            pltpu.VMEM((chunks, width, out_width), bf16),
            pltpu.VMEM((steps, 2, rows, 2 * width), bf16),
            pltpu.VMEM((steps, rows, 2 * width), bf16),
            pltpu.VMEM((steps, rows, 2 * width), bf16),
            pltpu.VMEM((steps, 2, rows, width), bf16),
            pltpu.VMEM((2 * rows, out_width), jnp.float32),
            pltpu.VMEM((groups, n_col, 2, piece, out_width), bf16),
            pltpu.VMEM((groups, n_col, 2, piece, out_width), bf16),
            dma((3, chunks)),
            dma((groups, n_col)),
            dma((groups, n_col)),
        ]
        + [dma((steps,))] * 8
        + [dma((groups, n_col))] * 2,
        compiler_params=pltpu.CompilerParams(
            collective_id=0, has_side_effects=True, vmem_limit_bytes=67043328
        ),
    )(acts.reshape(groups, 2, piece, depth), gate_weight, up_weight, down_weight)
    return out.reshape(tokens, out_width)


def solution(mesh):
    placed = (P("col", "row"), P("col", "row"), P("row", "col"), P("row", "col"), P("col", "row"))
    return jax.shard_map(
        functools.partial(on_device, mesh.shape["row"], mesh.shape["col"]),
        mesh=mesh,
        in_specs=placed,
        out_specs=P("col", "row"),
        check_vma=False,
    )
```

time: 237 us -> 126 us (0.53)
  waiting for transfers between devices: 176 us -> 0 us
  Pallas kernels: 0 us -> 121 us
  matrix products: 24.3 us -> 0 us
  blocking collectives: 14.2 us -> 0 us
  between operations: 13.2 us -> 0.02 us
  other arithmetic: 8.09 us -> 0.75 us
  local copies, waits for them, and re-layouts: 1.22 us -> 3.69 us
    reduce_scatter x2 -> x0, waiting for transfers between devices: 126 us -> none  [the longest x1 99.8 us: on_device(): lax.psum_scatter(jnp.concatenate([gate_part, up_part], axis=1).astype(jnp...]
    pallas_call x0 -> x1, Pallas kernels: none -> 121 us  [on_device(): pl.pallas_call(functools.partial(body, n_row, n_col), out_shape=jax.Shape...]
    all_gather x1 -> x0, waiting for transfers between devices: 49.8 us -> none  [on_device(): lax.all_gather(hidden, 'row', axis=0, tiled=True)]
    dot_general x3 -> x0, matrix products: 24.3 us -> none  [the longest x1 10.1 us: on_device(): jnp.dot(lax.all_gather(hidden, 'row', axis=0, tiled=True), down_weight, p...]
    all_gather x1 -> x0, blocking collectives: 14.2 us -> none  [on_device(): every = lax.all_gather(acts, 'col', axis=0, tiled=True)]
    concatenate x1 -> x0, other arithmetic: 4.77 us -> none  [on_device(): jnp.concatenate([gate_part, up_part], axis=1).astype(jnp.bfloat16)]
    convert_element_type x3 -> x1, other arithmetic: 3.32 us -> 0.75 us  [on_device(): (blocked * act_scales[:, :, None]).reshape(tokens, depth)]
  transfers between devices with their start and end apart: 3 -> 0, of which waited for: 3 -> 0; matrix products, arithmetic and copies ran while one was open for 0% -> 0% of each run, Pallas kernels for 0% -> 0%
where the time goes in v1:
time: 126 us
  Pallas kernels  121 us (96%)
  local copies, waits for them, and re-layouts  3.69 us (3%)
    pallas_call x1, Pallas kernels, on_device(): pl.pallas_call(functools.partial(body, n_row, n_col), out_shape=jax.Shape...  121 us
    unnamed x2, local copies, waits for them, and re-layouts  2.86 us

profile of v1, /device:TPU:0, one launch (start us, length us, event | category | flops | bytes accessed | tf_op | source)
XLA Modules:
  0.0 125.7 jit_solution(14585430256489481666)
XLA Ops:
  0.0 1.2 copy.7
  1.2 0.7 fusion
  2.0 0.8 copy.8
  2.8 121.3 %shard_map.55 = bf16[2,2,32,896]{3,2,1,0:T(8,128)(2,1)} custom-call(bf16[2,2,32,896]{3,2,1,0:T(8,128)(2,1)} %bitcast.6, bf16[896,4608]{1,0:T(8,128)(2,1)} %gate_hbm.1, bf16[896,4608]{1,0:T(8,128)(2,1)} %up_hbm.1, bf16[4608,896]{1,0:T(8,128)(2,1)} %down_hbm.1), custom_call_target="tpu_custom_call" | custom-call | tf_op jit(solution)/shard_map/pallas_call | solution.py:303
  124.1 1.6 %copy.10 = bf16[128,896]{1,0:T(8,128)(2,1)} copy(bf16[128,896]{1,0:T(8,128)(2,1)} %bitcast.7) | data formatting | bytes 458752
